TPU v7x, 256 devices: a whole 4x4x8 slice. The times are simulated.
256 devices in a mesh: band: 32 (over z, x_hi, core), lane: 8 (over y, x_lo).
Axes of the slice: x: 4 (x_hi: 2, x_lo: 2; x = x_hi * 2 + x_lo), y: 4, z: 8, core: 2. Of those that a mesh axis runs over, the one named last changes fastest.
Arguments:
- load_terms: float32 [2048, 512, 256], P('band', 'lane'), may hold values from -6 to 6
- start_values: float32 [2048, 512, 256], P('band', 'lane'), may hold values from -6 to 6
- reaction_rate: float32 [2048, 512, 256], P('band', 'lane'), may hold values from 0.1 to 0.9
Outputs:
- solution: float32 [2048, 512, 256], P('band', 'lane')
- remaining: float32 [2048, 512, 256], P('band', 'lane')
All inputs are finite; a program needn't handle non-finite values.
Results may differ from a plain program's by a relative error of at most 0.0003.
Values sent between devices are 32-bit elements.
A program may use at most 128 MiB of HBM per device.

v0:
```python
import functools

import jax
import jax.numpy as jnp
from jax import lax
from jax.experimental import pallas as pl
from jax.experimental.pallas import tpu as pltpu
from jax.sharding import PartitionSpec as P

BEFORE = 3
AFTER = 2
INNER = 13
OMEGA = 0.8
LANES = 128
DEPTH = 4
PAD = 8
CX = 16
MESH = pl.DeviceIdType.MESH


def kernel(
    bands, lanes, load_hbm, start_hbm, rate_hbm, sol_hbm, rem_hbm,
    u, f, w, diag, pair, cu, cl, cw, col_out, col_in, ccol_out, ccol_in, crow_in,
    in_sem, out_sem, send_sem, recv_sem, csend_sem, crecv_sem,
):
    ny, nx = f.shape[1], f.shape[2]
    my, mx = ny // 2, nx // 2
    chunks = f.shape[0]
    wide = mx + 2 * PAD
    band, lane = lax.axis_index("band"), lax.axis_index("lane")
    near = (
        (band > 0, {"band": band - 1}),
        (band < bands - 1, {"band": band + 1}),
        (lane > 0, {"lane": lane - 1}),
        (lane < lanes - 1, {"lane": lane + 1}),
    )
    fine_x = pl.ds(PAD, nx)

    def loads(c):
        part = pl.ds(c * LANES, LANES)
        return (
            pltpu.make_async_copy(start_hbm.at[:, :, part], u.at[0, c, pl.ds(1, ny), fine_x], in_sem.at[c, 0]),
            pltpu.make_async_copy(rate_hbm.at[:, :, part], diag.at[c], in_sem.at[c, 1]),
            pltpu.make_async_copy(load_hbm.at[:, :, part], f.at[c], in_sem.at[c, 2]),
        )

    def stores(c):
        part = pl.ds(c * LANES, LANES)
        final = (BEFORE + 1 + AFTER) % 2
        return (
            pltpu.make_async_copy(u.at[final, c, pl.ds(1, ny), fine_x], sol_hbm.at[:, :, part], out_sem.at[c, 0]),
            pltpu.make_async_copy(w.at[c], rem_hbm.at[:, :, part], out_sem.at[c, 1]),
        )

    for at in (0, 1, 2):
        for c in range(chunks):
            loads(c)[at].start()

    barrier = pltpu.get_barrier_semaphore()
    count = 0
    for there, device in near:
        count = count + there.astype(jnp.int32)

    zero_col = jnp.zeros((PAD, LANES), jnp.float32)
    for slot in range(2):
        for c in range(chunks):
            for y in (0, ny + 1):
                u[slot, c, y] = jnp.zeros(u.shape[3:], jnp.float32)

    @pl.loop(1, ny + 1)
    def _(y):
        for slot in range(2):
            for c in range(chunks):
                u[slot, c, y, 0:PAD, :] = zero_col
                u[slot, c, y, PAD + nx : 2 * PAD + nx, :] = zero_col

    @pl.loop(0, my + 2 * DEPTH)
    def _(y):
        zero_row = jnp.zeros(cu.shape[3:], jnp.float32)
        for c in range(chunks):
            cu[0, c, y] = zero_row
            cu[1, c, y] = zero_row
            cl[c, y] = zero_row
            cw[c, y] = zero_row

    for there, device in near:

        @pl.when(there)
        def _():
            pl.semaphore_signal(barrier, inc=1, device_id=device, device_id_type=MESH)

    pl.semaphore_wait(barrier, count)

    def fine_copy(k, c, side, device):
        p, o = k % 2, side ^ 1
        if side < 2:
            src = u.at[p, c, 1 if side == 0 else ny, fine_x]
            dst = u.at[p, c, ny + 1 if side == 0 else 0, fine_x]
        else:
            src = col_out.at[p, c, side - 2]
            dst = col_in.at[p, c, o - 2]
        return pltpu.make_async_remote_copy(
            src_ref=src, dst_ref=dst, send_sem=send_sem.at[p, c, side], recv_sem=recv_sem.at[p, c, o],
            device_id=device, device_id_type=MESH,
        )

    def send_fine(k, c):
        p = k % 2

        @pl.loop(0, ny, unroll=8)
        def _(y):
            col_out[p, c, 0, pl.ds(y, 1), :] = u[p, c, 1 + y, PAD : PAD + 1, :]
            col_out[p, c, 1, pl.ds(y, 1), :] = u[p, c, 1 + y, PAD + nx - 1 : PAD + nx, :]

        for side in (2, 3, 0, 1):
            there, device = near[side]

            @pl.when(there)
            def _():
                fine_copy(k, c, side, device).start()

    def wait_fine(k, c):
        p = k % 2
        for side in (0, 1, 2, 3):
            there, device = near[side]

            @pl.when(there)
            def _():
                fine_copy(k, c, side, device).wait_send()
                fine_copy(k, c, side ^ 1, device).wait_recv()
                if side >= 2:
                    at = PAD - 1 if side == 2 else PAD + nx

                    @pl.loop(0, ny, unroll=8)
                    def _(y):
                        u[p, c, 1 + y, at : at + 1, :] = col_in[p, c, side - 2, pl.ds(y, 1), :]

    def cross(ref, y, x, rows):
        middle = [ref[y + i - 1, pl.ds(x, 8), :] for i in range(rows + 2)]
        return [
            (
                middle[i + 1],
                (middle[i] + middle[i + 2])
                + (ref[y + i, pl.ds(x - 1, 8), :] + ref[y + i, pl.ds(x + 1, 8), :]),
            )
            for i in range(rows)
        ]

    def sweep_fine(k, c):
        src, dst, ff, ww = u.at[k % 2, c], u.at[(k + 1) % 2, c], f.at[c], w.at[c]
        rows = 4

        @pl.loop(0, ny // rows)
        def _(g):
            y = g * rows
            for x in range(0, nx, 8):
                for i, (here, total) in enumerate(cross(src, y + 1, PAD + x, rows)):
                    new = (1.0 - OMEGA) * here + ww[y + i, pl.ds(x, 8), :] * (ff[y + i, pl.ds(x, 8), :] + total)
                    dst[y + 1 + i, pl.ds(PAD + x, 8), :] = new

    def halve(slot):
        return pair[slot, pl.ds(0, mx, stride=2), :] + pair[slot, pl.ds(1, mx, stride=2), :]

    def prepare(c):
        @pl.loop(0, my)
        def _(j):
            y = 2 * j
            for x in range(0, nx, 8):
                part = pl.ds(x, 8)
                m0, m1 = diag[c, y, part, :], diag[c, y + 1, part, :]
                pair[c, part, :] = m0 + m1
                d0, d1 = 4.0 + m0, 4.0 + m1
                diag[c, y, part, :] = d0
                diag[c, y + 1, part, :] = d1
                w[c, y, part, :] = OMEGA / d0
                w[c, y + 1, part, :] = OMEGA / d1
            cw[c, DEPTH + j, CX : CX + mx, :] = OMEGA / (4.0 + 0.5 * halve(c))

    def restrict(k, c):
        src = u.at[k % 2, c]

        @pl.loop(0, my)
        def _(j):
            y = 2 * j
            for x in range(0, nx, 8):
                part = pl.ds(x, 8)
                both = [
                    f[c, y + i, part, :] + total - diag[c, y + i, part, :] * here
                    for i, (here, total) in enumerate(cross(src, y + 1, PAD + x, 2))
                ]
                pair[c, part, :] = both[0] + both[1]
            cl[c, DEPTH + j, CX : CX + mx, :] = 0.5 * halve(c)

    def coarse_ref(slot, c):
        return (cw.at[c], cl.at[c])[slot] if slot < 2 else cu.at[0, c]

    def coarse_copy(slot, c, side, device):
        o = side ^ 1
        if side < 2:
            src = coarse_ref(slot, c).at[pl.ds(DEPTH if side == 0 else my, DEPTH), pl.ds(CX - PAD, wide)]
            dst = crow_in.at[slot, c, o]
        else:
            src = ccol_out.at[slot, c, side - 2]
            dst = ccol_in.at[slot, c, o - 2]
        return pltpu.make_async_remote_copy(
            src_ref=src, dst_ref=dst, send_sem=csend_sem.at[slot, c, side], recv_sem=crecv_sem.at[slot, c, o],
            device_id=device, device_id_type=MESH,
        )

    def send_columns(slot, c):
        ref = coarse_ref(slot, c)

        @pl.loop(0, my, unroll=8)
        def _(y):
            ccol_out[slot, c, 0, pl.ds(y * DEPTH, DEPTH), :] = ref[DEPTH + y, CX : CX + DEPTH, :]
            ccol_out[slot, c, 1, pl.ds(y * DEPTH, DEPTH), :] = ref[DEPTH + y, CX + mx - DEPTH : CX + mx, :]

        for side in (2, 3):
            there, device = near[side]

            @pl.when(there)
            def _():
                coarse_copy(slot, c, side, device).start()

    def columns_then_rows(slot, c):
        ref = coarse_ref(slot, c)
        for side in (2, 3):
            there, device = near[side]

            @pl.when(there)
            def _():
                coarse_copy(slot, c, side, device).wait_send()
                coarse_copy(slot, c, side ^ 1, device).wait_recv()
                at = CX - DEPTH if side == 2 else CX + mx

                @pl.loop(0, my, unroll=8)
                def _(y):
                    ref[DEPTH + y, at : at + DEPTH, :] = ccol_in[slot, c, side - 2, pl.ds(y * DEPTH, DEPTH), :]

        for side in (0, 1):
            there, device = near[side]

            @pl.when(there)
            def _():
                coarse_copy(slot, c, side, device).start()

    def wait_rows(slot, c):
        ref = coarse_ref(slot, c)
        for side in (0, 1):
            there, device = near[side]
            at = 0 if side == 0 else DEPTH + my

            @pl.when(there)
            def _():
                coarse_copy(slot, c, side, device).wait_send()
                coarse_copy(slot, c, side ^ 1, device).wait_recv()
                for i in range(DEPTH):
                    ref[at + i, pl.ds(CX - PAD, wide), :] = crow_in[slot, c, side, i]

    def sweep_coarse(s, c):
        src, dst, ff, ww = cu.at[s % 2, c], cu.at[(s + 1) % 2, c], cl.at[c], cw.at[c]
        rows = 2
        first, number = s + 1, my + 2 * DEPTH - 2 * (s + 1)

        @pl.loop(0, number // rows)
        def _(g):
            y = first + g * rows
            for x in range(CX - PAD, CX - PAD + wide, 8):
                for i, (here, total) in enumerate(cross(src, y, x, rows)):
                    part = pl.ds(x, 8)
                    dst[y + i, part, :] = (1.0 - OMEGA) * here + ww[y + i, part, :] * (ff[y + i, part, :] + total)

    def first_coarse(c):
        @pl.loop(0, my + 2 * DEPTH)
        def _(y):
            part = pl.ds(CX - PAD, wide)
            cu[0, c, y, part, :] = cw[c, y, part, :] * cl[c, y, part, :]

    def correct(k, c):
        @pl.loop(0, my)
        def _(j):
            add = cu[0, c, DEPTH + j, CX : CX + mx, :]
            for i in range(2):
                for odd in range(2):
                    part = pl.ds(PAD + odd, mx, stride=2)
                    u[(k + 1) % 2, c, 1 + 2 * j + i, part, :] = u[k % 2, c, 1 + 2 * j + i, part, :] + add

    def leave(k, c):
        src = u.at[k % 2, c]
        rows = 4

        @pl.loop(0, ny // rows)
        def _(g):
            y = g * rows
            for x in range(0, nx, 8):
                part = pl.ds(x, 8)
                for i, (here, total) in enumerate(cross(src, y + 1, PAD + x, rows)):
                    w[c, y + i, part, :] = f[c, y + i, part, :] + total - diag[c, y + i, part, :] * here

    both = range(chunks)
    for c in both:
        loads(c)[0].wait()
        send_fine(0, c)
    for c in both:
        loads(c)[1].wait()
        prepare(c)
        send_columns(0, c)
    for c in both:
        loads(c)[2].wait()
    k = 0
    for sweep in range(BEFORE):
        for c in both:
            wait_fine(k, c)
            sweep_fine(k, c)
            send_fine(k + 1, c)
            if sweep == 0:
                columns_then_rows(0, c)
            if sweep == 1:
                wait_rows(0, c)
        k += 1
    for c in both:
        wait_fine(k, c)
        restrict(k, c)
        send_columns(1, c)
    for c in both:
        columns_then_rows(1, c)
    rounds = (INNER - 1) // DEPTH
    for turn in range(rounds):
        for c in both:
            wait_rows(1 + turn, c)
            if turn == 0:
                first_coarse(c)
            for s in range(DEPTH):
                sweep_coarse(s, c)
            if turn < rounds - 1:
                send_columns(2 + turn, c)
            else:
                correct(k, c)
                send_fine(k + 1, c)
        if turn < rounds - 1:
            for c in both:
                columns_then_rows(2 + turn, c)
    k += 1
    for sweep in range(AFTER):
        for c in both:
            wait_fine(k, c)
            sweep_fine(k, c)
            send_fine(k + 1, c)
            if sweep == AFTER - 1:
                stores(c)[0].start()
        k += 1
    for c in both:
        wait_fine(k, c)
        leave(k, c)
        stores(c)[1].start()
    for c in both:
        for copy in stores(c):
            copy.wait()


def solution(mesh):
    bands, lanes = mesh.shape["band"], mesh.shape["lane"]

    def on_device(load_terms, start_values, reaction_rate):
        ny, nx, layers = load_terms.shape
        chunks = layers // LANES
        my, mx = ny // 2, nx // 2
        slots = 1 + (INNER - 1) // DEPTH
        f32 = jnp.float32
        vmem = lambda *shape: pltpu.VMEM(shape + (LANES,), f32)
        dma = lambda *shape: pltpu.SemaphoreType.DMA(shape)
        return pl.pallas_call(
            functools.partial(kernel, bands, lanes),
            out_shape=[jax.ShapeDtypeStruct(load_terms.shape, f32)] * 2,
            in_specs=[pl.BlockSpec(memory_space=pl.ANY)] * 3,
            out_specs=[pl.BlockSpec(memory_space=pl.ANY)] * 2,
            scratch_shapes=[
                vmem(2, chunks, ny + 2, nx + 2 * PAD),
                vmem(chunks, ny, nx),
                vmem(chunks, ny, nx),
                vmem(chunks, ny, nx),
                vmem(chunks, nx),
                vmem(2, chunks, my + 2 * DEPTH, mx + 2 * CX),
                vmem(chunks, my + 2 * DEPTH, mx + 2 * CX),
                vmem(chunks, my + 2 * DEPTH, mx + 2 * CX),
                vmem(2, chunks, 2, ny),
                vmem(2, chunks, 2, ny),
                vmem(slots, chunks, 2, my * DEPTH),
                vmem(slots, chunks, 2, my * DEPTH),
                vmem(slots, chunks, 2, DEPTH, mx + 2 * PAD),
                dma(chunks, 3),
                dma(chunks, 2),
                dma(2, chunks, 4),
                dma(2, chunks, 4),
                dma(slots, chunks, 4),
                dma(slots, chunks, 4),
            ],
            compiler_params=pltpu.CompilerParams(
                collective_id=0, has_side_effects=True, vmem_limit_bytes=60 * 1024 * 1024
            ),
        )(load_terms, start_values, reaction_rate)

    placed = P("band", "lane", None)
    return jax.shard_map(
        on_device, mesh=mesh, in_specs=(placed,) * 3, out_specs=(placed, placed), check_vma=False
    )
```

profile of v0, /device:TPU:121, one launch (start us, length us, event | category | flops | bytes accessed | tf_op | source)
XLA Modules:
  0.0 100.3 jit_solution(1215201816394040511)
XLA Ops:
  0.6 92.7 %shard_map.50 = (f32[64,64,256]{2,1,0:T(8,128)}, f32[64,64,256]{2,1,0:T(8,128)}) custom-call(f32[64,64,256]{2,1,0:T(8,128)} %load_hbm.1, f32[64,64,256]{2,1,0:T(8,128)} %start_hbm.1, f32[64,64,256]{2,1,0:T(8,128)} %rate_hbm.1), custom_call_target="tpu_custom_call" | custom-call | tf_op jit(solution)/shard_map/pallas_call | solution.py:372
  93.4 0.0 copy-start
  93.4 4.8 %copy.7 = f32[64,64,256]{2,1,0:T(8,128)} copy(f32[64,64,256]{2,1,0:T(8,128)} %get-tuple-element.4) | data formatting | bytes 8388608
  98.2 0.0 copy-done
  98.2 2.0 %copy.8 = f32[64,64,256]{2,1,0:T(8,128)} copy(f32[64,64,256]{2,1,0:T(8,128)S(1)} %copy-done) | data formatting | bytes 8388608
Async XLA Ops:
  93.4 4.9 %copy-start = (f32[64,64,256]{2,1,0:T(8,128)S(1)}, f32[64,64,256]{2,1,0:T(8,128)}, u32[]{:S(2)}) copy-start(f32[64,64,256]{2,1,0:T(8,128)} %get-tuple-element.5) | copy-start | bytes 12582916
where the time goes:
time: 102 us; the launch traced here: 100 us
  Pallas kernels  92.7 us (91%)
  local copies, waits for them, and re-layouts  6.87 us (7%)
    pallas_call x1, Pallas kernels, on_device(): pl.pallas_call(functools.partial(kernel, bands, lanes), out_shape=[jax.Sh...  92.7 us
    unnamed x4, local copies, waits for them, and re-layouts  6.87 us

commit v1 on v0

--- a/solution.py
+++ b/solution.py
@@ -19,9 +19,9 @@
 
 
 def kernel(
-    bands, lanes, load_hbm, start_hbm, rate_hbm, sol_hbm, rem_hbm,
-    u, f, w, diag, pair, cu, cl, cw, col_out, col_in, ccol_out, ccol_in, crow_in,
-    in_sem, out_sem, send_sem, recv_sem, csend_sem, crecv_sem,
+    bands, lanes, load_hbm, start_hbm, rate_hbm, u, w,
+    f, diag, pair, cu, cl, cw, col_out, col_in, ccol_out, ccol_in, crow_in,
+    in_sem, send_sem, recv_sem, csend_sem, crecv_sem,
 ):
     ny, nx = f.shape[1], f.shape[2]
     my, mx = ny // 2, nx // 2
@@ -42,14 +42,6 @@
             pltpu.make_async_copy(start_hbm.at[:, :, part], u.at[0, c, pl.ds(1, ny), fine_x], in_sem.at[c, 0]),
             pltpu.make_async_copy(rate_hbm.at[:, :, part], diag.at[c], in_sem.at[c, 1]),
             pltpu.make_async_copy(load_hbm.at[:, :, part], f.at[c], in_sem.at[c, 2]),
-        )
-
-    def stores(c):
-        part = pl.ds(c * LANES, LANES)
-        final = (BEFORE + 1 + AFTER) % 2
-        return (
-            pltpu.make_async_copy(u.at[final, c, pl.ds(1, ny), fine_x], sol_hbm.at[:, :, part], out_sem.at[c, 0]),
-            pltpu.make_async_copy(w.at[c], rem_hbm.at[:, :, part], out_sem.at[c, 1]),
         )
 
     for at in (0, 1, 2):
@@ -346,16 +338,24 @@
             wait_fine(k, c)
             sweep_fine(k, c)
             send_fine(k + 1, c)
-            if sweep == AFTER - 1:
-                stores(c)[0].start()
         k += 1
     for c in both:
         wait_fine(k, c)
         leave(k, c)
-        stores(c)[1].start()
-    for c in both:
-        for copy in stores(c):
-            copy.wait()
+
+
+def store_kernel(u, w, sol_hbm, rem_hbm, out_sem):
+    chunks, ny, nx = w.shape[:3]
+    final = (BEFORE + 1 + AFTER) % 2
+    copies = []
+    for c in range(chunks):
+        part = pl.ds(c * LANES, LANES)
+        copies.append(pltpu.make_async_copy(u.at[final, c, pl.ds(1, ny), pl.ds(PAD, nx)], sol_hbm.at[:, :, part], out_sem.at[c, 0]))
+        copies.append(pltpu.make_async_copy(w.at[c], rem_hbm.at[:, :, part], out_sem.at[c, 1]))
+    for copy in copies:
+        copy.start()
+    for copy in copies:
+        copy.wait()
 
 
 def solution(mesh):
@@ -369,14 +369,12 @@
         f32 = jnp.float32
         vmem = lambda *shape: pltpu.VMEM(shape + (LANES,), f32)
         dma = lambda *shape: pltpu.SemaphoreType.DMA(shape)
-        return pl.pallas_call(
+        u, w = pl.pallas_call(
             functools.partial(kernel, bands, lanes),
-            out_shape=[jax.ShapeDtypeStruct(load_terms.shape, f32)] * 2,
+            out_shape=[vmem(2, chunks, ny + 2, nx + 2 * PAD), vmem(chunks, ny, nx)],
             in_specs=[pl.BlockSpec(memory_space=pl.ANY)] * 3,
-            out_specs=[pl.BlockSpec(memory_space=pl.ANY)] * 2,
+            out_specs=[pl.BlockSpec(memory_space=pltpu.VMEM)] * 2,
             scratch_shapes=[
-                vmem(2, chunks, ny + 2, nx + 2 * PAD),
-                vmem(chunks, ny, nx),
                 vmem(chunks, ny, nx),
                 vmem(chunks, ny, nx),
                 vmem(chunks, nx),
@@ -389,16 +387,23 @@
                 vmem(slots, chunks, 2, my * DEPTH),
                 vmem(slots, chunks, 2, DEPTH, mx + 2 * PAD),
                 dma(chunks, 3),
-                dma(chunks, 2),
                 dma(2, chunks, 4),
                 dma(2, chunks, 4),
                 dma(slots, chunks, 4),
                 dma(slots, chunks, 4),
             ],
             compiler_params=pltpu.CompilerParams(
-                collective_id=0, has_side_effects=True, vmem_limit_bytes=60 * 1024 * 1024
+                collective_id=0, has_side_effects=True, vmem_limit_bytes=46 * 1024 * 1024
             ),
         )(load_terms, start_values, reaction_rate)
+        return pl.pallas_call(
+            store_kernel,
+            out_shape=[jax.ShapeDtypeStruct(load_terms.shape, f32)] * 2,
+            in_specs=[pl.BlockSpec(memory_space=pltpu.VMEM)] * 2,
+            out_specs=[pl.BlockSpec(memory_space=pl.ANY)] * 2,
+            scratch_shapes=[dma(chunks, 2)],
+            compiler_params=pltpu.CompilerParams(vmem_limit_bytes=1024 * 1024),
+        )(pltpu.with_memory_space_constraint(u, pltpu.VMEM), pltpu.with_memory_space_constraint(w, pltpu.VMEM))
 
     placed = P("band", "lane", None)
     return jax.shard_map(

time: 102 us -> 97.2 us (0.953)
  local copies, waits for them, and re-layouts: 6.87 us -> 0 us
  Pallas kernels: 92.7 us -> 94.7 us
    unnamed x4 -> x0, local copies, waits for them, and re-layouts: 6.87 us -> none
    pallas_call x1 -> x2, Pallas kernels: 92.7 us -> 94.7 us  [the longest x1 91.3 us: on_device(): pl.pallas_call(functools.partial(kernel, bands, lanes), out_shape=[vmem(2...]
where the time goes in v1:
time: 97.2 us; the launch traced here: 95.4 us
  Pallas kernels  94.7 us (97%)
    pallas_call x1, Pallas kernels, on_device(): pl.pallas_call(functools.partial(kernel, bands, lanes), out_shape=[vmem(2...  91.3 us
    pallas_call x1, Pallas kernels, on_device(): pl.pallas_call(store_kernel, out_shape=[jax.ShapeDtypeStruct(load_terms.s...  3.37 us

profile of v1, /device:TPU:121, one launch (start us, length us, event | category | flops | bytes accessed | tf_op | source)
XLA Modules:
  0.0 95.4 jit_solution(11634454746942813869)
XLA Ops:
  0.6 91.3 %shard_map.50 = (f32[2,2,66,80,128]{4,3,2,1,0:T(8,128)S(1)}, f32[2,64,64,128]{3,2,1,0:T(8,128)S(1)}) custom-call(f32[64,64,256]{2,1,0:T(8,128)} %load_hbm.1, f32[64,64,256]{2,1,0:T(8,128)} %start_hbm.1, f32[64,64,256]{2,1,0:T(8,128)} %rate_hbm.1), custom_call_target="tpu_custom_call" | custom-call | tf_op jit(solution)/shard_map/pallas_call | solution.py:372
  92.0 3.4 %shard_map.51 = (f32[64,64,256]{2,1,0:T(8,128)}, f32[64,64,256]{2,1,0:T(8,128)}) custom-call(f32[2,2,66,80,128]{4,3,2,1,0:T(8,128)S(1)} %get-tuple-element.4.u, f32[2,64,64,128]{3,2,1,0:T(8,128)S(1)} %get-tuple-element.5.w), custom_call_target="tpu_custom_call" | custom-call | tf_op jit(solution)/shard_map/pallas_call | solution.py:399

commit v2 on v1

v2 whole, which is shorter than its diff:
```python
import functools

import jax
import jax.numpy as jnp
from jax import lax
from jax.experimental import pallas as pl
from jax.experimental.pallas import tpu as pltpu
from jax.sharding import PartitionSpec as P

BEFORE = 3
AFTER = 2
INNER = 13
OMEGA = 0.8
LANES = 128
DEPTH = 4
ROUNDS = (INNER - 1) // DEPTH
DEPTHS = (DEPTH,) * ROUNDS + (DEPTH + 1,)
PAD = 8
CX = 16
RY = DEPTH + 1
FINAL = (BEFORE + AFTER) % 2
MESH = pl.DeviceIdType.MESH


def corner_rows(depth):
    return -(-depth * (depth - 1) // 8) * 8


def opposite(side):
    return side ^ 1 if side < 4 else 11 - side


def kernel(
    bands, lanes, load_hbm, start_hbm, rate_hbm, u, w,
    f, diag, pair, cu, cl, cw, col_out, col_in, ccol_out, ccol_in, crow_in, corner_in,
    in_sem, send_sem, recv_sem, csend_sem, crecv_sem,
):
    ny, nx = f.shape[1], f.shape[2]
    my, mx = ny // 2, nx // 2
    chunks = f.shape[0]
    both = range(chunks)
    band, lane = lax.axis_index("band"), lax.axis_index("lane")
    near = [
        (band > 0, {"band": band - 1}),
        (band < bands - 1, {"band": band + 1}),
        (lane > 0, {"lane": lane - 1}),
        (lane < lanes - 1, {"lane": lane + 1}),
    ]
    for side in range(2):
        for across in range(2, 4):
            near.append((near[side][0] & near[across][0], near[side][1] | near[across][1]))
    fine_x = pl.ds(PAD, nx)

    def loads(c):
        part = pl.ds(c * LANES, LANES)
        return (
            pltpu.make_async_copy(start_hbm.at[:, :, part], u.at[0, c, pl.ds(1, ny), fine_x], in_sem.at[c, 0]),
            pltpu.make_async_copy(rate_hbm.at[:, :, part], diag.at[c], in_sem.at[c, 1]),
            pltpu.make_async_copy(load_hbm.at[:, :, part], f.at[c], in_sem.at[c, 2]),
        )

    barrier = pltpu.get_barrier_semaphore()
    count = 0
    for there, device in near:
        count = count + there.astype(jnp.int32)

    for at in (0, 1, 2):
        for c in both:
            loads(c)[at].start()

    zero = jnp.zeros((8, LANES), jnp.float32)
    for slot in range(2):
        for c in both:
            for y in (0, ny + 1):
                u[slot, c, y] = jnp.zeros(u.shape[3:], jnp.float32)

    for there, device in near:

        @pl.when(there)
        def _():
            pl.semaphore_signal(barrier, inc=1, device_id=device, device_id_type=MESH)

    @pl.loop(1, ny + 1)
    def _(y):
        for slot in range(2):
            for c in both:
                u[slot, c, y, 0:PAD, :] = zero
                u[slot, c, y, PAD + nx : 2 * PAD + nx, :] = zero

    @pl.loop(0, my + 2 * RY)
    def _(y):
        zero_row = jnp.zeros(cu.shape[3:], jnp.float32)
        for c in both:
            cu[0, c, y] = zero_row
            cu[1, c, y] = zero_row
            cl[c, y] = zero_row
            cw[c, y] = zero_row

    pl.semaphore_wait(barrier, count)

    def fine_copy(k, c, side, device):
        p, o = k % 2, opposite(side)
        if side < 2:
            src = u.at[p, c, 1 if side == 0 else ny, fine_x]
            dst = u.at[p, c, ny + 1 if side == 0 else 0, fine_x]
        else:
            src = col_out.at[p, c, side - 2]
            dst = col_in.at[p, c, o - 2]
        return pltpu.make_async_remote_copy(
            src_ref=src, dst_ref=dst, send_sem=send_sem.at[p, c, side], recv_sem=recv_sem.at[p, c, o],
            device_id=device, device_id_type=MESH,
        )

    def start_fine(k, c, sides):
        for side in sides:
            there, device = near[side]

            @pl.when(there)
            def _():
                fine_copy(k, c, side, device).start()

    def send_fine(k, c):
        p = k % 2
        start_fine(k, c, (0, 1))

        @pl.loop(0, ny, unroll=8)
        def _(y):
            col_out[p, c, 0, pl.ds(y, 1), :] = u[p, c, 1 + y, PAD : PAD + 1, :]
            col_out[p, c, 1, pl.ds(y, 1), :] = u[p, c, 1 + y, PAD + nx - 1 : PAD + nx, :]

        start_fine(k, c, (2, 3))

    def wait_fine(k, c):
        p = k % 2
        for side in (2, 3, 0, 1):
            there, device = near[side]

            @pl.when(there)
            def _():
                fine_copy(k, c, side, device).wait_send()
                fine_copy(k, c, opposite(side), device).wait_recv()
                if side >= 2:
                    at = PAD - 1 if side == 2 else PAD + nx

                    @pl.loop(0, ny, unroll=8)
                    def _(y):
                        u[p, c, 1 + y, at : at + 1, :] = col_in[p, c, side - 2, pl.ds(y, 1), :]

    def cross(ref, y, x, rows):
        middle = [ref[y + i - 1, pl.ds(x, 8), :] for i in range(rows + 2)]
        return [
            (
                middle[i + 1],
                (middle[i] + middle[i + 2])
                + (ref[y + i, pl.ds(x - 1, 8), :] + ref[y + i, pl.ds(x + 1, 8), :]),
            )
            for i in range(rows)
        ]

    def over(first, last, rows, body):
        groups = (last - first) // rows

        @pl.loop(0, groups)
        def _(g):
            body(first + g * rows, rows)

        if (last - first) % rows:
            body(first + groups * rows, (last - first) % rows)

    def outer(step, c):
        edges = (0, nx - 8)
        over(0, ny, 4, lambda y, rows: step(c, y, edges, rows))
        for y in (0, ny - 1):
            step(c, y, range(8, nx - 8, 8), 1)

    def inner(step, c):
        over(1, ny - 1, 4, lambda y, rows: step(c, y, range(8, nx - 8, 8), rows))

    def smooth(k):
        def step(c, y, xs, rows):
            src, dst, ff, ww = u.at[k % 2, c], u.at[(k + 1) % 2, c], f.at[c], w.at[c]
            for x in xs:
                for i, (here, total) in enumerate(cross(src, y + 1, PAD + x, rows)):
                    new = (1.0 - OMEGA) * here + ww[y + i, pl.ds(x, 8), :] * (ff[y + i, pl.ds(x, 8), :] + total)
                    dst[y + 1 + i, pl.ds(PAD + x, 8), :] = new

        return step

    def leave(k):
        def step(c, y, xs, rows):
            src = u.at[k % 2, c]
            for x in xs:
                part = pl.ds(x, 8)
                for i, (here, total) in enumerate(cross(src, y + 1, PAD + x, rows)):
                    w[c, y + i, part, :] = f[c, y + i, part, :] + total - diag[c, y + i, part, :] * here

        return step

    def halve(slot):
        return pair[slot, pl.ds(0, mx, stride=2), :] + pair[slot, pl.ds(1, mx, stride=2), :]

    def prepare(c):
        @pl.loop(0, my)
        def _(j):
            y = 2 * j
            for x in range(0, nx, 8):
                part = pl.ds(x, 8)
                m0, m1 = diag[c, y, part, :], diag[c, y + 1, part, :]
                pair[c, part, :] = m0 + m1
                d0, d1 = 4.0 + m0, 4.0 + m1
                diag[c, y, part, :] = d0
                diag[c, y + 1, part, :] = d1
                w[c, y, part, :] = OMEGA / d0
                w[c, y + 1, part, :] = OMEGA / d1
            cw[c, RY + j, CX : CX + mx, :] = OMEGA / (4.0 + 0.5 * halve(c))

    def restrict(k, c, first, last):
        src = u.at[k % 2, c]

        @pl.loop(first, last)
        def _(j):
            y = 2 * j
            for x in range(0, nx, 8):
                part = pl.ds(x, 8)
                both = [
                    f[c, y + i, part, :] + total - diag[c, y + i, part, :] * here
                    for i, (here, total) in enumerate(cross(src, y + 1, PAD + x, 2))
                ]
                pair[c, part, :] = both[0] + both[1]
            cl[c, RY + j, CX : CX + mx, :] = 0.5 * halve(c)

    def coarse_ref(slot, c):
        return (cw.at[c], cl.at[c])[slot] if slot < 2 else cu.at[0, c]

    def coarse_copy(slot, c, side, device):
        d, o = DEPTHS[slot], opposite(side)
        if side < 2:
            src = coarse_ref(slot, c).at[pl.ds(RY if side == 0 else RY + my - d, d), pl.ds(CX, mx)]
            dst = crow_in.at[slot, c, o, pl.ds(0, d)]
        elif side < 4:
            src = ccol_out.at[slot, c, side - 2, pl.ds(0, my * d)]
            dst = ccol_in.at[slot, c, o - 2, pl.ds(0, my * d)]
        else:
            number = corner_rows(d)
            src = ccol_out.at[slot, c, side % 2, pl.ds(0 if side < 6 else my * d - number, number)]
            dst = corner_in.at[slot, c, o - 4, pl.ds(0, number)]
        return pltpu.make_async_remote_copy(
            src_ref=src, dst_ref=dst, send_sem=csend_sem.at[slot, c, side], recv_sem=crecv_sem.at[slot, c, o],
            device_id=device, device_id_type=MESH,
        )

    def start_coarse(slot, c, sides):
        for side in sides:
            there, device = near[side]

            @pl.when(there)
            def _():
                coarse_copy(slot, c, side, device).start()

    def send_rows(slot, c):
        start_coarse(slot, c, (0, 1))

    def send_columns(slot, c):
        ref, d = coarse_ref(slot, c), DEPTHS[slot]

        @pl.loop(0, my, unroll=8)
        def _(y):
            ccol_out[slot, c, 0, pl.ds(y * d, d), :] = ref[RY + y, CX : CX + d, :]
            ccol_out[slot, c, 1, pl.ds(y * d, d), :] = ref[RY + y, CX + mx - d : CX + mx, :]

        start_coarse(slot, c, (4, 5, 6, 7, 2, 3))

    def wait_coarse(slot, c):
        ref, d = coarse_ref(slot, c), DEPTHS[slot]
        number = corner_rows(d)
        for side in range(8):
            there, device = near[side]

            @pl.when(there)
            def _():
                coarse_copy(slot, c, side, device).wait_send()
                coarse_copy(slot, c, opposite(side), device).wait_recv()
                if side < 2:
                    for i in range(d):
                        ref[(RY - d if side == 0 else RY + my) + i, pl.ds(CX, mx), :] = crow_in[slot, c, side, i]
                elif side < 4:
                    at = CX - d if side == 2 else CX + mx

                    @pl.loop(0, my, unroll=8)
                    def _(y):
                        ref[RY + y, at : at + d, :] = ccol_in[slot, c, side - 2, pl.ds(y * d, d), :]
                else:
                    at = CX - d if side % 2 == 0 else CX + mx
                    for i in range(1, d):
                        row, start = (RY - i, number - i * d) if side < 6 else (RY + my + i - 1, (i - 1) * d)
                        ref[row, at : at + d, :] = corner_in[slot, c, side - 4, start : start + d, :]

    coarse_x = range(CX - DEPTH, CX + mx + DEPTH, 8)

    def sweep_coarse(s, c, first, last):
        src, dst, ff, ww = cu.at[s % 2, c], cu.at[(s + 1) % 2, c], cl.at[c], cw.at[c]

        def step(y, rows):
            for x in coarse_x:
                for i, (here, total) in enumerate(cross(src, y, x, rows)):
                    part = pl.ds(x, 8)
                    dst[y + i, part, :] = (1.0 - OMEGA) * here + ww[y + i, part, :] * (ff[y + i, part, :] + total)

        over(RY + first, RY + last, 2, step)

    def first_coarse(c):
        @pl.loop(RY - DEPTH, RY + my + DEPTH)
        def _(y):
            for x in coarse_x:
                part = pl.ds(x, 8)
                cu[0, c, y, part, :] = cw[c, y, part, :] * cl[c, y, part, :]

    def correct(k, c):
        p = k % 2

        def rows(add, ys):
            for y in ys:
                for odd in range(2):
                    part = pl.ds(PAD + odd, mx, stride=2)
                    u[p, c, y, part, :] = u[p, c, y, part, :] + add

        @pl.loop(0, my)
        def _(j):
            y = 1 + 2 * j
            rows(cu[0, c, RY + j, CX : CX + mx, :], (y, y + 1))
            for at, beside in ((PAD - 1, CX - 1), (PAD + nx, CX + mx)):
                add = cu[0, c, RY + j, beside : beside + 1, :]
                for i in range(2):
                    u[p, c, y + i, at : at + 1, :] = u[p, c, y + i, at : at + 1, :] + add

        rows(cu[0, c, RY - 1, CX : CX + mx, :], (0,))
        rows(cu[0, c, RY + my, CX : CX + mx, :], (ny + 1,))

    for c in both:
        loads(c)[0].wait()
        send_fine(0, c)
    for c in both:
        loads(c)[1].wait()
        prepare(c)
        send_rows(0, c)
        send_columns(0, c)
    for c in both:
        loads(c)[2].wait()
    for k in range(BEFORE):
        for c in both:
            wait_fine(k, c)
            outer(smooth(k), c)
            send_fine(k + 1, c)
            inner(smooth(k), c)
    k = BEFORE
    for c in both:
        wait_fine(k, c)
        restrict(k, c, 0, DEPTH)
        restrict(k, c, my - DEPTH, my)
        send_rows(1, c)
        restrict(k, c, DEPTH, my - DEPTH)
        send_columns(1, c)
    for turn in range(ROUNDS):
        slot = 1 + turn
        for c in both:
            if turn == 0:
                wait_coarse(0, c)
            wait_coarse(slot, c)
            if turn == 0:
                first_coarse(c)
            reach = DEPTHS[slot] - 1
            for s in range(DEPTH - 1):
                sweep_coarse(s, c, s - reach, my + reach - s)
            if turn < ROUNDS - 1:
                d = DEPTHS[slot + 1]
                sweep_coarse(DEPTH - 1, c, 0, d)
                sweep_coarse(DEPTH - 1, c, my - d, my)
                send_rows(slot + 1, c)
                sweep_coarse(DEPTH - 1, c, d, my - d)
                send_columns(slot + 1, c)
            else:
                sweep_coarse(DEPTH - 1, c, -1, my + 1)
                correct(k, c)
                outer(smooth(k), c)
                send_fine(k + 1, c)
                inner(smooth(k), c)
    for k in range(BEFORE + 1, BEFORE + AFTER):
        for c in both:
            wait_fine(k, c)
            outer(smooth(k), c)
            send_fine(k + 1, c)
            inner(smooth(k), c)
            if k == BEFORE + AFTER - 1:
                inner(leave(k + 1), c)
    for c in both:
        wait_fine(BEFORE + AFTER, c)
        outer(leave(BEFORE + AFTER), c)


def store_kernel(u, w, sol_hbm, rem_hbm, out_sem):
    chunks, ny, nx = w.shape[:3]
    copies = []
    for c in range(chunks):
        part = pl.ds(c * LANES, LANES)
        values = u.at[FINAL, c, pl.ds(1, ny), pl.ds(PAD, nx)]
        copies.append(pltpu.make_async_copy(values, sol_hbm.at[:, :, part], out_sem.at[c, 0]))
        copies.append(pltpu.make_async_copy(w.at[c], rem_hbm.at[:, :, part], out_sem.at[c, 1]))
    for copy in copies:
        copy.start()
    for copy in copies:
        copy.wait()


def solution(mesh):
    bands, lanes = mesh.shape["band"], mesh.shape["lane"]

    def on_device(load_terms, start_values, reaction_rate):
        ny, nx, layers = load_terms.shape
        chunks = layers // LANES
        my, mx = ny // 2, nx // 2
        slots = ROUNDS + 1
        f32 = jnp.float32
        vmem = lambda *shape: pltpu.VMEM(shape + (LANES,), f32)
        dma = lambda *shape: pltpu.SemaphoreType.DMA(shape)
        u, w = pl.pallas_call(
            functools.partial(kernel, bands, lanes),
            out_shape=[vmem(2, chunks, ny + 2, nx + 2 * PAD), vmem(chunks, ny, nx)],
            in_specs=[pl.BlockSpec(memory_space=pl.ANY)] * 3,
            out_specs=[pl.BlockSpec(memory_space=pltpu.VMEM)] * 2,
            scratch_shapes=[
                vmem(chunks, ny, nx),
                vmem(chunks, ny, nx),
                vmem(chunks, nx),
                vmem(2, chunks, my + 2 * RY, mx + 2 * CX),
                vmem(chunks, my + 2 * RY, mx + 2 * CX),
                vmem(chunks, my + 2 * RY, mx + 2 * CX),
                vmem(2, chunks, 2, ny),
                vmem(2, chunks, 2, ny),
                vmem(slots, chunks, 2, my * RY),
                vmem(slots, chunks, 2, my * RY),
                vmem(slots, chunks, 2, RY, mx),
                vmem(slots, chunks, 4, corner_rows(RY)),
                dma(chunks, 3),
                dma(2, chunks, 4),
                dma(2, chunks, 4),
                dma(slots, chunks, 8),
                dma(slots, chunks, 8),
            ],
            compiler_params=pltpu.CompilerParams(
                collective_id=0, has_side_effects=True, vmem_limit_bytes=46 * 1024 * 1024
            ),
        )(load_terms, start_values, reaction_rate)
        in_vmem = lambda x: pltpu.with_memory_space_constraint(x, pltpu.VMEM)
        return pl.pallas_call(
            store_kernel,
            out_shape=[jax.ShapeDtypeStruct(load_terms.shape, f32)] * 2,
            in_specs=[pl.BlockSpec(memory_space=pltpu.VMEM)] * 2,
            out_specs=[pl.BlockSpec(memory_space=pl.ANY)] * 2,
            scratch_shapes=[dma(chunks, 2)],
            compiler_params=pltpu.CompilerParams(vmem_limit_bytes=1024 * 1024),
        )(in_vmem(u), in_vmem(w))

    placed = P("band", "lane", None)
    return jax.shard_map(
        on_device, mesh=mesh, in_specs=(placed,) * 3, out_specs=(placed, placed), check_vma=False
    )
```

time: 97.2 us -> 86.1 us (0.89); the launches traced: 95.4 us -> 86.1 us
  Pallas kernels: 94.7 us -> 85.4 us
    pallas_call x1, Pallas kernels: 91.3 us -> 82.1 us  [on_device(): pl.pallas_call(functools.partial(kernel, bands, lanes), out_shape=[vmem(2...]
where the time goes in v2:
time: 86.1 us
  Pallas kernels  85.4 us (99%)
    pallas_call x1, Pallas kernels, on_device(): pl.pallas_call(functools.partial(kernel, bands, lanes), out_shape=[vmem(2...  82.1 us
    pallas_call x1, Pallas kernels, on_device(): pl.pallas_call(store_kernel, out_shape=[jax.ShapeDtypeStruct(load_terms.s...  3.37 us

profile of v2, /device:TPU:121, one launch (start us, length us, event | category | flops | bytes accessed | tf_op | source)
XLA Modules:
  0.0 86.1 jit_solution(17196529534301449012)
XLA Ops:
  0.6 82.1 %shard_map.50 = (f32[2,2,66,80,128]{4,3,2,1,0:T(8,128)S(1)}, f32[2,64,64,128]{3,2,1,0:T(8,128)S(1)}) custom-call(f32[64,64,256]{2,1,0:T(8,128)} %load_hbm.1, f32[64,64,256]{2,1,0:T(8,128)} %start_hbm.1, f32[64,64,256]{2,1,0:T(8,128)} %rate_hbm.1), custom_call_target="tpu_custom_call" | custom-call | tf_op jit(solution)/shard_map/pallas_call | solution.py:425
  82.7 3.4 %shard_map.51 = (f32[64,64,256]{2,1,0:T(8,128)}, f32[64,64,256]{2,1,0:T(8,128)}) custom-call(f32[2,2,66,80,128]{4,3,2,1,0:T(8,128)S(1)} %get-tuple-element.4.u, f32[2,64,64,128]{3,2,1,0:T(8,128)S(1)} %get-tuple-element.5.w), custom_call_target="tpu_custom_call" | custom-call | tf_op jit(solution)/shard_map/pallas_call | solution.py:454

commit v3 on v2

--- a/solution.py
+++ b/solution.py
@@ -80,22 +80,6 @@
         def _():
             pl.semaphore_signal(barrier, inc=1, device_id=device, device_id_type=MESH)
 
-    @pl.loop(1, ny + 1)
-    def _(y):
-        for slot in range(2):
-            for c in both:
-                u[slot, c, y, 0:PAD, :] = zero
-                u[slot, c, y, PAD + nx : 2 * PAD + nx, :] = zero
-
-    @pl.loop(0, my + 2 * RY)
-    def _(y):
-        zero_row = jnp.zeros(cu.shape[3:], jnp.float32)
-        for c in both:
-            cu[0, c, y] = zero_row
-            cu[1, c, y] = zero_row
-            cl[c, y] = zero_row
-            cw[c, y] = zero_row
-
     pl.semaphore_wait(barrier, count)
 
     def fine_copy(k, c, side, device):
@@ -169,7 +153,7 @@
 
     def outer(step, c):
         edges = (0, nx - 8)
-        over(0, ny, 4, lambda y, rows: step(c, y, edges, rows))
+        over(0, ny, 8, lambda y, rows: step(c, y, edges, rows))
         for y in (0, ny - 1):
             step(c, y, range(8, nx - 8, 8), 1)
 
@@ -206,28 +190,31 @@
             for x in range(0, nx, 8):
                 part = pl.ds(x, 8)
                 m0, m1 = diag[c, y, part, :], diag[c, y + 1, part, :]
-                pair[c, part, :] = m0 + m1
+                pair[2 * c, part, :] = m0 + m1
                 d0, d1 = 4.0 + m0, 4.0 + m1
                 diag[c, y, part, :] = d0
                 diag[c, y + 1, part, :] = d1
                 w[c, y, part, :] = OMEGA / d0
                 w[c, y + 1, part, :] = OMEGA / d1
-            cw[c, RY + j, CX : CX + mx, :] = OMEGA / (4.0 + 0.5 * halve(c))
+            cw[c, RY + j, CX : CX + mx, :] = OMEGA / (4.0 + 0.5 * halve(2 * c))
 
     def restrict(k, c, first, last):
         src = u.at[k % 2, c]
 
-        @pl.loop(first, last)
-        def _(j):
+        def step(j, rows):
             y = 2 * j
             for x in range(0, nx, 8):
                 part = pl.ds(x, 8)
-                both = [
+                defect = [
                     f[c, y + i, part, :] + total - diag[c, y + i, part, :] * here
-                    for i, (here, total) in enumerate(cross(src, y + 1, PAD + x, 2))
+                    for i, (here, total) in enumerate(cross(src, y + 1, PAD + x, 2 * rows))
                 ]
-                pair[c, part, :] = both[0] + both[1]
-            cl[c, RY + j, CX : CX + mx, :] = 0.5 * halve(c)
+                for i in range(rows):
+                    pair[2 * c + i, part, :] = defect[2 * i] + defect[2 * i + 1]
+            for i in range(rows):
+                cl[c, RY + j + i, CX : CX + mx, :] = 0.5 * halve(2 * c + i)
+
+        over(first, last, 2, step)
 
     def coarse_ref(slot, c):
         return (cw.at[c], cl.at[c])[slot] if slot < 2 else cu.at[0, c]
@@ -306,44 +293,74 @@
                     part = pl.ds(x, 8)
                     dst[y + i, part, :] = (1.0 - OMEGA) * here + ww[y + i, part, :] * (ff[y + i, part, :] + total)
 
-        over(RY + first, RY + last, 2, step)
+        over(RY + first, RY + last, 4, step)
 
     def first_coarse(c):
-        @pl.loop(RY - DEPTH, RY + my + DEPTH)
+        @pl.loop(RY - DEPTH, RY + my + DEPTH, unroll=4)
         def _(y):
             for x in coarse_x:
                 part = pl.ds(x, 8)
                 cu[0, c, y, part, :] = cw[c, y, part, :] * cl[c, y, part, :]
 
-    def correct(k, c):
+    def correct(k, c, outside):
         p = k % 2
-
-        def rows(add, ys):
-            for y in ys:
-                for odd in range(2):
-                    part = pl.ds(PAD + odd, mx, stride=2)
-                    u[p, c, y, part, :] = u[p, c, y, part, :] + add
-
-        @pl.loop(0, my)
+        near_x, far_x = (0, mx - 8), range(8, mx - 8, 8)
+
+        def block(j, ys, xs):
+            for x in xs:
+                add = cu[0, c, RY + j, pl.ds(CX + x, 8), :]
+                for y in ys:
+                    for odd in range(2):
+                        part = pl.ds(PAD + 2 * x + odd, 8, stride=2)
+                        u[p, c, y, part, :] = u[p, c, y, part, :] + add
+
+        if not outside:
+
+            @pl.loop(1, my - 1, unroll=2)
+            def _(j):
+                block(j, (1 + 2 * j, 2 + 2 * j), far_x)
+
+            return
+
+        @pl.loop(0, my, unroll=2)
         def _(j):
             y = 1 + 2 * j
-            rows(cu[0, c, RY + j, CX : CX + mx, :], (y, y + 1))
+            block(j, (y, y + 1), near_x)
             for at, beside in ((PAD - 1, CX - 1), (PAD + nx, CX + mx)):
                 add = cu[0, c, RY + j, beside : beside + 1, :]
                 for i in range(2):
                     u[p, c, y + i, at : at + 1, :] = u[p, c, y + i, at : at + 1, :] + add
 
-        rows(cu[0, c, RY - 1, CX : CX + mx, :], (0,))
-        rows(cu[0, c, RY + my, CX : CX + mx, :], (ny + 1,))
+        block(-1, (0,), range(0, mx, 8))
+        block(0, (1, 2), far_x)
+        block(my - 1, (ny - 1, ny), far_x)
+        block(my, (ny + 1,), range(0, mx, 8))
+
+    def clear():
+        @pl.loop(1, ny + 1)
+        def _(y):
+            for slot in range(2):
+                for c in both:
+                    u[slot, c, y, 0:PAD, :] = zero
+                    u[slot, c, y, PAD + nx : 2 * PAD + nx, :] = zero
+
+        @pl.loop(0, my + 2 * RY)
+        def _(y):
+            zero_row = jnp.zeros(cu.shape[3:], jnp.float32)
+            for c in both:
+                cu[0, c, y] = zero_row
+                cu[1, c, y] = zero_row
+                cl[c, y] = zero_row
+                cw[c, y] = zero_row
 
     for c in both:
         loads(c)[0].wait()
         send_fine(0, c)
+    clear()
     for c in both:
         loads(c)[1].wait()
         prepare(c)
         send_rows(0, c)
-        send_columns(0, c)
     for c in both:
         loads(c)[2].wait()
     for k in range(BEFORE):
@@ -351,6 +368,8 @@
             wait_fine(k, c)
             outer(smooth(k), c)
             send_fine(k + 1, c)
+            if c == chunks - 1 and k < chunks:
+                send_columns(0, k)
             inner(smooth(k), c)
     k = BEFORE
     for c in both:
@@ -380,9 +399,10 @@
                 send_columns(slot + 1, c)
             else:
                 sweep_coarse(DEPTH - 1, c, -1, my + 1)
-                correct(k, c)
+                correct(k, c, True)
                 outer(smooth(k), c)
                 send_fine(k + 1, c)
+                correct(k, c, False)
                 inner(smooth(k), c)
     for k in range(BEFORE + 1, BEFORE + AFTER):
         for c in both:
@@ -430,7 +450,7 @@
             scratch_shapes=[
                 vmem(chunks, ny, nx),
                 vmem(chunks, ny, nx),
-                vmem(chunks, nx),
+                vmem(2 * chunks, nx),
                 vmem(2, chunks, my + 2 * RY, mx + 2 * CX),
                 vmem(chunks, my + 2 * RY, mx + 2 * CX),
                 vmem(chunks, my + 2 * RY, mx + 2 * CX),

time: 86.1 us -> 80.9 us (0.940)
  Pallas kernels: 85.4 us -> 79.5 us
    pallas_call x1, Pallas kernels: 82.1 us -> 76.1 us  [on_device(): pl.pallas_call(functools.partial(kernel, bands, lanes), out_shape=[vmem(2...]
where the time goes in v3:
time: 80.9 us; the launch traced here: 80.1 us
  Pallas kernels  79.5 us (98%)
    pallas_call x1, Pallas kernels, on_device(): pl.pallas_call(functools.partial(kernel, bands, lanes), out_shape=[vmem(2...  76.1 us
    pallas_call x1, Pallas kernels, on_device(): pl.pallas_call(store_kernel, out_shape=[jax.ShapeDtypeStruct(load_terms.s...  3.37 us

profile of v3, /device:TPU:121, one launch (start us, length us, event | category | flops | bytes accessed | tf_op | source)
XLA Modules:
  0.0 80.1 jit_solution(11730934425005990715)
XLA Ops:
  0.6 76.1 %shard_map.50 = (f32[2,2,66,80,128]{4,3,2,1,0:T(8,128)S(1)}, f32[2,64,64,128]{3,2,1,0:T(8,128)S(1)}) custom-call(f32[64,64,256]{2,1,0:T(8,128)} %load_hbm.1, f32[64,64,256]{2,1,0:T(8,128)} %start_hbm.1, f32[64,64,256]{2,1,0:T(8,128)} %rate_hbm.1), custom_call_target="tpu_custom_call" | custom-call | tf_op jit(solution)/shard_map/pallas_call | solution.py:445
  76.7 3.4 %shard_map.51 = (f32[64,64,256]{2,1,0:T(8,128)}, f32[64,64,256]{2,1,0:T(8,128)}) custom-call(f32[2,2,66,80,128]{4,3,2,1,0:T(8,128)S(1)} %get-tuple-element.4.u, f32[2,64,64,128]{3,2,1,0:T(8,128)S(1)} %get-tuple-element.5.w), custom_call_target="tpu_custom_call" | custom-call | tf_op jit(solution)/shard_map/pallas_call | solution.py:474

commit v4 on v3

--- a/solution.py
+++ b/solution.py
@@ -12,7 +12,7 @@
 INNER = 13
 OMEGA = 0.8
 LANES = 128
-DEPTH = 4
+DEPTH = 3
 ROUNDS = (INNER - 1) // DEPTH
 DEPTHS = (DEPTH,) * ROUNDS + (DEPTH + 1,)
 PAD = 8
@@ -103,9 +103,8 @@
             def _():
                 fine_copy(k, c, side, device).start()
 
-    def send_fine(k, c):
+    def send_columns_fine(k, c):
         p = k % 2
-        start_fine(k, c, (0, 1))
 
         @pl.loop(0, ny, unroll=8)
         def _(y):
@@ -114,14 +113,23 @@
 
         start_fine(k, c, (2, 3))
 
-    def wait_fine(k, c):
-        p = k % 2
-        for side in (2, 3, 0, 1):
+    def finish_fine(k, c):
+        for side in range(4):
             there, device = near[side]
 
             @pl.when(there)
             def _():
                 fine_copy(k, c, side, device).wait_send()
+
+    def wait_fine(k, c):
+        p = k % 2
+        if k not in (0, BEFORE + 1):
+            finish_fine(k - 1, c)
+        for side in (2, 3, 0, 1):
+            there, device = near[side]
+
+            @pl.when(there)
+            def _():
                 fine_copy(k, c, opposite(side), device).wait_recv()
                 if side >= 2:
                     at = PAD - 1 if side == 2 else PAD + nx
@@ -151,11 +159,12 @@
         if (last - first) % rows:
             body(first + groups * rows, (last - first) % rows)
 
-    def outer(step, c):
-        edges = (0, nx - 8)
-        over(0, ny, 8, lambda y, rows: step(c, y, edges, rows))
+    def outer_rows(step, c):
         for y in (0, ny - 1):
-            step(c, y, range(8, nx - 8, 8), 1)
+            step(c, y, range(0, nx, 8), 1)
+
+    def outer_columns(step, c):
+        over(1, ny - 1, 8, lambda y, rows: step(c, y, (0, nx - 8), rows))
 
     def inner(step, c):
         over(1, ny - 1, 4, lambda y, rows: step(c, y, range(8, nx - 8, 8), rows))
@@ -179,6 +188,16 @@
                     w[c, y + i, part, :] = f[c, y + i, part, :] + total - diag[c, y + i, part, :] * here
 
         return step
+
+    def sweep(k, c, between=None):
+        step = smooth(k)
+        outer_rows(step, c)
+        start_fine(k + 1, c, (0, 1))
+        outer_columns(step, c)
+        send_columns_fine(k + 1, c)
+        if between is not None:
+            between()
+        inner(step, c)
 
     def halve(slot):
         return pair[slot, pl.ds(0, mx, stride=2), :] + pair[slot, pl.ds(1, mx, stride=2), :]
@@ -217,7 +236,7 @@
         over(first, last, 2, step)
 
     def coarse_ref(slot, c):
-        return (cw.at[c], cl.at[c])[slot] if slot < 2 else cu.at[0, c]
+        return (cw.at[c], cl.at[c])[slot] if slot < 2 else cu.at[DEPTH * (slot - 1) % 2, c]
 
     def coarse_copy(slot, c, side, device):
         d, o = DEPTHS[slot], opposite(side)
@@ -265,7 +284,6 @@
 
             @pl.when(there)
             def _():
-                coarse_copy(slot, c, side, device).wait_send()
                 coarse_copy(slot, c, opposite(side), device).wait_recv()
                 if side < 2:
                     for i in range(d):
@@ -282,6 +300,14 @@
                         row, start = (RY - i, number - i * d) if side < 6 else (RY + my + i - 1, (i - 1) * d)
                         ref[row, at : at + d, :] = corner_in[slot, c, side - 4, start : start + d, :]
 
+    def finish_coarse(slot, c, sides):
+        for side in sides:
+            there, device = near[side]
+
+            @pl.when(there)
+            def _():
+                coarse_copy(slot, c, side, device).wait_send()
+
     coarse_x = range(CX - DEPTH, CX + mx + DEPTH, 8)
 
     def sweep_coarse(s, c, first, last):
@@ -355,7 +381,8 @@
 
     for c in both:
         loads(c)[0].wait()
-        send_fine(0, c)
+        start_fine(0, c, (0, 1))
+        send_columns_fine(0, c)
     clear()
     for c in both:
         loads(c)[1].wait()
@@ -366,11 +393,7 @@
     for k in range(BEFORE):
         for c in both:
             wait_fine(k, c)
-            outer(smooth(k), c)
-            send_fine(k + 1, c)
-            if c == chunks - 1 and k < chunks:
-                send_columns(0, k)
-            inner(smooth(k), c)
+            sweep(k, c, functools.partial(send_columns, 0, k) if c == chunks - 1 and k < chunks else None)
     k = BEFORE
     for c in both:
         wait_fine(k, c)
@@ -387,34 +410,37 @@
             wait_coarse(slot, c)
             if turn == 0:
                 first_coarse(c)
-            reach = DEPTHS[slot] - 1
+            reach, base = DEPTHS[slot] - 1, DEPTH * turn
             for s in range(DEPTH - 1):
-                sweep_coarse(s, c, s - reach, my + reach - s)
+                sweep_coarse(base + s, c, s - reach, my + reach - s)
+                if s == 0 and turn > 0:
+                    finish_coarse(slot, c, (0, 1))
             if turn < ROUNDS - 1:
                 d = DEPTHS[slot + 1]
-                sweep_coarse(DEPTH - 1, c, 0, d)
-                sweep_coarse(DEPTH - 1, c, my - d, my)
+                sweep_coarse(base + DEPTH - 1, c, 0, d)
+                sweep_coarse(base + DEPTH - 1, c, my - d, my)
                 send_rows(slot + 1, c)
-                sweep_coarse(DEPTH - 1, c, d, my - d)
+                sweep_coarse(base + DEPTH - 1, c, d, my - d)
                 send_columns(slot + 1, c)
             else:
-                sweep_coarse(DEPTH - 1, c, -1, my + 1)
+                sweep_coarse(base + DEPTH - 1, c, -1, my + 1)
+                finish_fine(k, c)
                 correct(k, c, True)
-                outer(smooth(k), c)
-                send_fine(k + 1, c)
-                correct(k, c, False)
-                inner(smooth(k), c)
+                sweep(k, c, functools.partial(correct, k, c, False))
     for k in range(BEFORE + 1, BEFORE + AFTER):
         for c in both:
             wait_fine(k, c)
-            outer(smooth(k), c)
-            send_fine(k + 1, c)
-            inner(smooth(k), c)
+            sweep(k, c)
             if k == BEFORE + AFTER - 1:
                 inner(leave(k + 1), c)
     for c in both:
         wait_fine(BEFORE + AFTER, c)
-        outer(leave(BEFORE + AFTER), c)
+        outer_rows(leave(BEFORE + AFTER), c)
+        outer_columns(leave(BEFORE + AFTER), c)
+    for c in both:
+        finish_fine(BEFORE + AFTER, c)
+        for slot in range(ROUNDS + 1):
+            finish_coarse(slot, c, range(8) if slot < 2 else range(2, 8))
 
 
 def store_kernel(u, w, sol_hbm, rem_hbm, out_sem):

time: 80.9 us -> 77.9 us (0.963)
  Pallas kernels: 79.5 us -> 77.1 us
    pallas_call x1, Pallas kernels: 76.1 us -> 73.8 us  [on_device(): pl.pallas_call(functools.partial(kernel, bands, lanes), out_shape=[vmem(2...]
where the time goes in v4:
time: 77.9 us; the launch traced here: 77.8 us
  Pallas kernels  77.1 us (99%)
    pallas_call x1, Pallas kernels, on_device(): pl.pallas_call(functools.partial(kernel, bands, lanes), out_shape=[vmem(2...  73.8 us
    pallas_call x1, Pallas kernels, on_device(): pl.pallas_call(store_kernel, out_shape=[jax.ShapeDtypeStruct(load_terms.s...  3.37 us

profile of v4, /device:TPU:121, one launch (start us, length us, event | category | flops | bytes accessed | tf_op | source)
XLA Modules:
  0.0 77.8 jit_solution(4465142494836928798)
XLA Ops:
  0.6 73.8 %shard_map.50 = (f32[2,2,66,80,128]{4,3,2,1,0:T(8,128)S(1)}, f32[2,64,64,128]{3,2,1,0:T(8,128)S(1)}) custom-call(f32[64,64,256]{2,1,0:T(8,128)} %load_hbm.1, f32[64,64,256]{2,1,0:T(8,128)} %start_hbm.1, f32[64,64,256]{2,1,0:T(8,128)} %rate_hbm.1), custom_call_target="tpu_custom_call" | custom-call | tf_op jit(solution)/shard_map/pallas_call | solution.py:471
  74.4 3.4 %shard_map.51 = (f32[64,64,256]{2,1,0:T(8,128)}, f32[64,64,256]{2,1,0:T(8,128)}) custom-call(f32[2,2,66,80,128]{4,3,2,1,0:T(8,128)S(1)} %get-tuple-element.4.u, f32[2,64,64,128]{3,2,1,0:T(8,128)S(1)} %get-tuple-element.5.w), custom_call_target="tpu_custom_call" | custom-call | tf_op jit(solution)/shard_map/pallas_call | solution.py:500

commit v5 on v4

--- a/solution.py
+++ b/solution.py
@@ -263,18 +263,25 @@
             def _():
                 coarse_copy(slot, c, side, device).start()
 
+    def pack_columns(slot, c, y):
+        ref, d = coarse_ref(slot, c), DEPTHS[slot]
+        ccol_out[slot, c, 0, pl.ds(y * d, d), :] = ref[RY + y, CX : CX + d, :]
+        ccol_out[slot, c, 1, pl.ds(y * d, d), :] = ref[RY + y, CX + mx - d : CX + mx, :]
+
     def send_rows(slot, c):
-        start_coarse(slot, c, (0, 1))
+        d = DEPTHS[slot]
+        for y in (*range(d), *range(my - d, my)):
+            pack_columns(slot, c, y)
+        start_coarse(slot, c, (4, 5, 6, 7, 0, 1))
 
     def send_columns(slot, c):
-        ref, d = coarse_ref(slot, c), DEPTHS[slot]
-
-        @pl.loop(0, my, unroll=8)
+        d = DEPTHS[slot]
+
+        @pl.loop(d, my - d, unroll=2)
         def _(y):
-            ccol_out[slot, c, 0, pl.ds(y * d, d), :] = ref[RY + y, CX : CX + d, :]
-            ccol_out[slot, c, 1, pl.ds(y * d, d), :] = ref[RY + y, CX + mx - d : CX + mx, :]
-
-        start_coarse(slot, c, (4, 5, 6, 7, 2, 3))
+            pack_columns(slot, c, y)
+
+        start_coarse(slot, c, (2, 3))
 
     def wait_coarse(slot, c):
         ref, d = coarse_ref(slot, c), DEPTHS[slot]

time: 77.9 us -> 79.3 us (1.018)
  Pallas kernels: 77.1 us -> 78.6 us
    pallas_call x1, Pallas kernels: 73.8 us -> 75.2 us  [on_device(): pl.pallas_call(functools.partial(kernel, bands, lanes), out_shape=[vmem(2...]
where the time goes in v5:
time: 79.3 us; the launch traced here: 79.2 us
  Pallas kernels  78.6 us (99%)
    pallas_call x1, Pallas kernels, on_device(): pl.pallas_call(functools.partial(kernel, bands, lanes), out_shape=[vmem(2...  75.2 us
    pallas_call x1, Pallas kernels, on_device(): pl.pallas_call(store_kernel, out_shape=[jax.ShapeDtypeStruct(load_terms.s...  3.37 us

profile of v5, /device:TPU:121, one launch (start us, length us, event | category | flops | bytes accessed | tf_op | source)
XLA Modules:
  0.0 79.2 jit_solution(13431698009339189968)
XLA Ops:
  0.6 75.2 %shard_map.50 = (f32[2,2,66,80,128]{4,3,2,1,0:T(8,128)S(1)}, f32[2,64,64,128]{3,2,1,0:T(8,128)S(1)}) custom-call(f32[64,64,256]{2,1,0:T(8,128)} %load_hbm.1, f32[64,64,256]{2,1,0:T(8,128)} %start_hbm.1, f32[64,64,256]{2,1,0:T(8,128)} %rate_hbm.1), custom_call_target="tpu_custom_call" | custom-call | tf_op jit(solution)/shard_map/pallas_call | solution.py:478
  75.8 3.4 %shard_map.51 = (f32[64,64,256]{2,1,0:T(8,128)}, f32[64,64,256]{2,1,0:T(8,128)}) custom-call(f32[2,2,66,80,128]{4,3,2,1,0:T(8,128)S(1)} %get-tuple-element.4.u, f32[2,64,64,128]{3,2,1,0:T(8,128)S(1)} %get-tuple-element.5.w), custom_call_target="tpu_custom_call" | custom-call | tf_op jit(solution)/shard_map/pallas_call | solution.py:507
